TPU v7x, 8 devices: a whole 2x2x1 slice. The times are simulated.
8 devices in a mesh: fsdp: 8 (over z, y, x, core).
Axes of the slice: x: 2, y: 2, z: 1, core: 2. Of those that a mesh axis runs over, the one named last changes fastest.
Arguments:
- left_mat: bfloat16 [49152, 2560], P('fsdp')
- right_mat: bfloat16 [2560, 2560], P('fsdp')
Outputs:
- output: bfloat16 [49152, 2560], P('fsdp')
All inputs are finite; a program needn't handle non-finite values.
Results may differ from a plain program's by a relative error of at most 0.001.
Values are sent between devices in bfloat16 or wider.
A program may use at most 1 GiB of HBM per device.

v0:
```python
import jax
import jax.numpy as jnp
from jax import lax
from jax.sharding import PartitionSpec as P


def solution(mesh):
    spec_rows = P("fsdp", None)

    def local_fn(left_blk, right_blk):
        full_right = lax.all_gather(right_blk, "fsdp", axis=0, tiled=True)
        return jnp.dot(left_blk, full_right, preferred_element_type=jnp.float32).astype(jnp.bfloat16)

    return jax.shard_map(local_fn, mesh=mesh, in_specs=(spec_rows, spec_rows), out_specs=spec_rows, check_vma=False)
```

profile of v0, /device:TPU:0, one launch (start us, length us, event | category | flops | bytes accessed | tf_op | source)
XLA Modules:
  0.0 177.6 jit_solution(11390437379682045190)
XLA Ops:
  6.5 0.0 all-gather.2.cloned.1.call-start
  6.5 0.7 all-gather.2.cloned.1.call-update
  7.3 73.3 %all-gather.2.cloned.1.call-done = bf16[2560,2560]{1,0:T(8,128)(2,1)} async-done(((bf16[320,2560]{1,0:T(8,128)(2,1)}), bf16[2560,2560]{1,0:T(8,128)(2,1)}) %all-gather.2.cloned.1.call-update) | async-done | bytes 13107216 | tf_op jit(solution)/shard_map/all_gather | solution.py:11
  80.5 90.2 %convolution_convert_fusion = bf16[6144,2560]{1,0:T(8,128)(2,1)} fusion(bf16[6144,2560]{1,0:T(8,128)(2,1)} %param.2, bf16[2560,2560]{1,0:T(8,128)(2,1)} %all-gather.2.cloned.1.call-done), kind=kOutput, calls=%fused_computation | convolution fusion | flops 80546365440 | bytes 76021760 | tf_op jit(solution)/shard_map/dot_general | solution.py:12
Async XLA Ops:
  6.5 74.0 %all-gather.2.cloned.1.call-start = ((), (), s32[]{:S(2)}) async-start(), calls=%async_computation | async-start | bytes 14745600 | tf_op jit(solution)/shard_map/all_gather | solution.py:11
Sparse Core Ops, SparseCore 0:
  9.1 71.3 all-gather.1
where the time goes:
time: 178 us
  matrix products  90.2 us (51%)
  waiting for transfers between devices  74 us (42%)
  between operations  13.4 us (8%)
    dot_general x1, matrix products, local_fn(): jnp.dot(left_blk, full_right, preferred_element_type=jnp.float32)  90.2 us
    all_gather x1, waiting for transfers between devices, local_fn(): full_right = lax.all_gather(right_blk, 'fsdp', axis=0, tiled=True)  73.3 us
  transfers between devices with their start and end apart: 1, of which 1 were waited for; matrix products, arithmetic and copies ran while one was open for 0% of the time, Pallas kernels for 0%

commit v1 on v0

v1 whole, which is shorter than its diff:
```python
import jax
import jax.numpy as jnp
from jax import lax
from jax.experimental import pallas as pl
from jax.experimental.pallas import tpu as pltpu
from jax.sharding import PartitionSpec as P

MESH = pl.DeviceIdType.MESH
BF16 = jnp.bfloat16
F32 = jnp.float32
ROWS = 6144
SLAB = 1024
SLABS = ROWS // SLAB
TRIP = 3 * SLAB
DEPTH = 2560
KT = 256
PW = 256
PANELS = 10
BLK = 320
HALF = BLK // 2
PART = 128
FIRST = 7
ACCP = 3
GRANT = int(21.4 * 2**20)


def _place():
    me = lax.axis_index("fsdp")
    core = me % 2
    x = (me // 2) % 2
    y = me // 4
    return me, core, x, y


def _ktiles():
    _, _, x, y = _place()
    own, other = 5 * y, 5 * (1 - y)
    return (
        [own + 3 * x + i for i in range(2)]
        + [own + 2 * (1 - x) + i for i in range(3)]
        + [other + 3 * x + i for i in range(2)]
        + [other + 2 * (1 - x) + i for i in range(3)]
    )


class Mxu:
    def __init__(self, accs, abuf, bbuf):
        self.accs, self.abuf, self.bbuf = accs, abuf, bbuf
        self.kt = _ktiles()

    def acc(self, rng, q, p):
        return self.accs[(rng * 2 + q) * 4 + p]

    def push(self, panel, i, reg):
        rows = pl.ds(pl.multiple_of(self.kt[i] * KT, KT), KT)
        for q in range(2):
            pltpu.matmul_push_rhs(self.bbuf[panel, rows, :], staging_register=reg, mxu_index=q)

    def drop(self, reg):
        zero = jnp.zeros((PART, KT), BF16)
        for q in range(2):
            pltpu.matmul_acc_lhs(self.acc(0, q, 0), zero, load_staged_rhs=reg)

    def clear(self):
        for r in self.accs:
            pltpu.matmul_pop(r)

    def tile(self, rng, slab, panel, nextpanel, poss, start_reg, emit):
        n = len(poss)
        reg = start_reg
        pieces = [(p, q) for p in range(4) for q in range(2)]
        slots = 4 if n > 4 else n - 1
        per = -(-len(pieces) // max(slots, 1))
        for k, i in enumerate(poss):
            for q in range(2):
                for p in range(4):
                    rows = pl.ds(pl.multiple_of(slab * SLAB + q * 512 + p * PART, PART), PART)
                    pltpu.matmul_acc_lhs(
                        self.acc(rng, q, p), self.abuf[i, rows, :], load_staged_rhs=reg if p == 0 else None
                    )
            reg = 1 - reg
            if k < n - 1:
                self.push(panel, poss[k + 1], reg)
            else:
                self.push(nextpanel, poss[0], reg)
            if k >= 1:
                for p, q in pieces[(k - 1) * per : k * per]:
                    emit(q * 512 + p * PART, pltpu.matmul_pop(self.acc(1 - rng, q, p)))
        return reg

    def drain(self, rng, emit):
        for p in range(4):
            for q in range(2):
                emit(q * 512 + p * PART, pltpu.matmul_pop(self.acc(rng, q, p)))


def _kernel1(a_ref, b_ref, abuf, bbuf, c1_ref, psum, stage, asem, bsem, osem, ssem, rsem, psem):
    me, core, x, y = _place()
    xn = 4 * y + 2 * (1 - x) + core
    yn = 4 * (1 - y) + 2 * x + core
    dn = 4 * (1 - y) + 2 * (1 - x) + core
    other = 4 * y + 2 * x + (1 - core)
    oxn = 4 * y + 2 * (1 - x) + (1 - core)
    oyn = 4 * (1 - y) + 2 * x + (1 - core)
    odn = 4 * (1 - y) + 2 * (1 - x) + (1 - core)
    kt = _ktiles()

    def rows(dev, part=0, size=BLK):
        return pl.ds(pl.multiple_of(dev * BLK + part * HALF, 32), size)

    def remote(kind, n, sl, dev):
        piece = bbuf.at[n, sl]
        return pltpu.make_async_remote_copy(
            src_ref=piece, dst_ref=piece, send_sem=ssem.at[kind, n], recv_sem=rsem.at[kind, n],
            device_id=(dev,), device_id_type=MESH,
        )

    send = {
        0: lambda n: remote(0, n, rows(me), xn),
        1: lambda n: remote(1, n, rows(me), yn),
        2: lambda n: remote(2, n, rows(xn, 0, HALF), yn),
        3: lambda n: remote(3, n, rows(yn, 1, HALF), xn),
        4: lambda n: remote(4, n, rows(xn), other),
        5: lambda n: remote(5, n, rows(yn), other),
        6: lambda n: remote(6, n, rows(dn), other),
    }
    recv = {
        0: lambda n: remote(0, n, rows(xn), xn),
        1: lambda n: remote(1, n, rows(yn), yn),
        2: lambda n: remote(2, n, rows(dn, 0, HALF), yn),
        3: lambda n: remote(3, n, rows(dn, 1, HALF), xn),
        4: lambda n: remote(4, n, rows(oxn), other),
        5: lambda n: remote(5, n, rows(oyn), other),
        6: lambda n: remote(6, n, rows(odn), other),
    }

    def pair(part, dev):
        lo, size = ((0, ACCP), (ACCP, PANELS - ACCP))[part]
        piece = bbuf.at[pl.ds(lo, size), rows(dev)]
        return pltpu.make_async_remote_copy(
            src_ref=piece, dst_ref=piece, send_sem=psem.at[0, part], recv_sem=psem.at[1, part],
            device_id=(other,), device_id_type=MESH,
        )

    def aload(i):
        cols = pl.ds(pl.multiple_of(kt[i] * KT, KT), KT)
        return pltpu.make_async_copy(a_ref.at[:, cols], abuf.at[i], asem.at[i])

    def bload(n):
        return pltpu.make_async_copy(b_ref.at[:, pl.ds(n * PW, PW)], bbuf.at[n, rows(me)], bsem.at[n])

    def arrived(n):
        recv[0](n).wait_recv()
        recv[1](n).wait_recv()
        for kind in (2, 3, 4, 5):
            send[kind](n).start()

    def ahead(n):
        send[0](n).start()
        send[1](n).start()

    def diagonal(n):
        recv[2](n).wait_recv()
        recv[3](n).wait_recv()
        send[6](n).start()

    def service1(n):
        arrived(n)
        ahead(n + 2)

    def xy_ready(n):
        recv[4](n).wait_recv()
        recv[5](n).wait_recv()

    def d_ready(n):
        recv[6](n).wait_recv()

    def product(n, row, poss):
        total = None
        for i in poss:
            left = abuf[i, pl.ds(pl.multiple_of(row, SLAB), SLAB), :]
            right = bbuf[n, pl.ds(pl.multiple_of(kt[i] * KT, KT), KT), :]
            part = jnp.dot(left, right, preferred_element_type=F32)
            total = part if total is None else total + part
        return total

    def out_copy(g, panel, t):
        return pltpu.make_async_copy(
            stage.at[g % 2], c1_ref.at[panel, pl.ds(pl.multiple_of(t * TRIP, TRIP), TRIP)], osem.at[g % 2]
        )

    def keep(n, poss, slot, t, add=False):
        for s in range(3):
            row = t * TRIP + s * SLAB
            at = slice(s * SLAB, (s + 1) * SLAB)
            value = product(n, row, poss)
            psum[slot, at, :] = psum[slot, at, :] + value if add else value

    def final(n, poss, slot, t):
        g = 2 * n + t

        @pl.when(g >= 2)
        def _():
            out_copy(g, 0, 0).wait()

        for s in range(3):
            row = t * TRIP + s * SLAB
            value = product(n, row, poss)
            if slot is not None:
                value = psum[slot, s * SLAB : (s + 1) * SLAB, :] + value
            stage[g % 2, s * SLAB : (s + 1) * SLAB, :] = value.astype(BF16)
        out_copy(g, n, t).start()

    def halves(body, between=None):
        def trip(t, _):
            if between is not None:
                pl.when(t == 1)(between)
            body(t)
            return 0

        lax.fori_loop(0, 2, trip, 0)

    for n in range(PANELS):
        bload(n).start()
    for i in range(2):
        aload(i).start()
    barrier = pltpu.get_barrier_semaphore()
    for dev in (other, xn, yn):
        pl.semaphore_signal(barrier, inc=1, device_id=(dev,), device_id_type=MESH)
    pl.semaphore_wait(barrier, 3)
    bload(0).wait()
    ahead(0)
    bload(1).wait()
    bload(2).wait()
    pair(0, me).start()
    ahead(1)
    for n in range(3, PANELS):
        bload(n).wait()
    pair(1, me).start()

    own, mid, far = [0, 1], [2, 3, 4, 5, 6], [7, 8, 9]
    aload(0).wait()
    aload(1).wait()
    for i in range(2, 10):
        aload(i).start()
    pair(0, other).wait_recv()

    def own_half(v, _):
        @pl.when(v == 4)
        def _():
            service1(0)

        keep(v // 2, own, v, v % 2)
        return 0

    lax.fori_loop(0, 5, own_half, 0)
    for i in range(2, 7):
        aload(i).wait()
    xy_ready(0)
    halves(lambda t: keep(0, mid, t, t, True))
    service1(1)
    diagonal(0)
    xy_ready(1)
    halves(lambda t: keep(1, mid, 2 + t, t, True))
    service1(2)
    for i in range(7, 10):
        aload(i).wait()
    d_ready(0)
    halves(lambda t: final(0, far, t, t))
    diagonal(1)
    xy_ready(2)
    keep(2, mid, 4, 0, True)
    service1(3)
    d_ready(1)
    halves(lambda t: final(1, far, 2 + t, t), lambda: diagonal(2))
    d_ready(2)
    final(2, far, 4, 0)
    final(2, own + mid + far, None, 1)
    service1(4)
    xy_ready(3)
    pair(1, other).wait_recv()
    halves(lambda t: keep(3, own + mid, t, t), lambda: diagonal(3))
    service1(5)
    d_ready(3)
    halves(lambda t: final(3, far, t, t), lambda: diagonal(4))

    def full_half(u, _):
        n, t = 4 + u // 2, u % 2

        @pl.when(t == 0)
        def _():
            xy_ready(n)
            d_ready(n)

        @pl.when((u >= 1) & (u <= 2))
        def _():
            service1(5 + u)
            diagonal(4 + u)

        @pl.when(u == 3)
        def _():
            arrived(8)

        @pl.when(u == 4)
        def _():
            diagonal(7)

        @pl.when(u == 5)
        def _():
            arrived(9)
            diagonal(8)

        final(n, own + mid + far, None, t)
        return 0

    lax.fori_loop(0, 2 * (FIRST - 4), full_half, 0)
    diagonal(9)
    for n in range(FIRST, PANELS):
        xy_ready(n)
        d_ready(n)
    for kind in range(7):
        for n in range(PANELS):
            send[kind](n).wait_send()
    for part in range(2):
        pair(part, me).wait_send()
    for g in range(2):
        out_copy(g, 0, 0).wait()


def _kernel2(abuf, bbuf, c1_ref, c_ref, stage, move, osem, lsem, wsem, *accs):
    mxu = Mxu(accs, abuf, bbuf)
    trips = (PANELS - FIRST) * SLABS // 2
    poss = list(range(10))

    def load(u):
        return pltpu.make_async_copy(c1_ref.at[u], move.at[u % 3], lsem.at[u % 3])

    def store(u):
        cols = pl.ds(pl.multiple_of(u * PW, PW), PW)
        return pltpu.make_async_copy(move.at[u % 3], c_ref.at[:, cols], wsem.at[u % 3])

    def out_copy(tau):
        panel = FIRST + tau // SLABS
        return pltpu.make_async_copy(
            stage.at[tau % 4],
            c_ref.at[
                pl.ds(pl.multiple_of((tau % SLABS) * SLAB, SLAB), SLAB), pl.ds(pl.multiple_of(panel * PW, PW), PW)
            ],
            osem.at[tau % 4],
        )

    load(0).start()
    mxu.clear()
    mxu.push(FIRST, 0, 0)

    def trip(u, _):
        @pl.when((u >= 1) & (u <= FIRST))
        def _():
            load(u - 1).wait()
            store(u - 1).start()

        @pl.when((u >= 3) & (u <= FIRST + 2))
        def _():
            store(u - 3).wait()

        @pl.when((u >= 1) & (u < FIRST))
        def _():
            load(u).start()

        for j in range(2):
            tau = 2 * u + j - 1

            @pl.when(tau >= 4)
            def _():
                out_copy(tau - 4).wait()

        reg = 0
        for j in range(2):
            tau = 2 * u + j
            panel = FIRST + tau // SLABS
            nextpanel = FIRST + ((tau + 1) // SLABS) % (PANELS - FIRST)

            def emit(row, value, slot=(tau + 3) % 4):
                stage[slot, pl.ds(row, PART), :] = value.astype(BF16)

            reg = mxu.tile(j, tau % SLABS, panel, nextpanel, poss, reg, emit)

        @pl.when(u > 0)
        def _():
            out_copy(2 * u - 1).start()

        out_copy(2 * u).start()
        return 0

    lax.fori_loop(0, trips, trip, 0)
    last = 2 * trips - 1
    out_copy(last - 4).wait()

    def emit(row, value):
        stage[last % 4, pl.ds(row, PART), :] = value.astype(BF16)

    mxu.drain(1, emit)
    out_copy(last).start()
    mxu.drop(0)
    for u in range(trips - 3, FIRST):
        store(u).wait()
    for tau in range(last - 3, last + 1):
        out_copy(tau).wait()


def _with_accs(kernel):
    def run(*refs):
        specs = [pltpu.ACC(q)((PART, PW), F32) for _ in range(2) for q in range(2) for _ in range(4)]
        pl.run_scoped(lambda *accs: kernel(*refs, *accs), *specs)

    return run


def _local(a, b):
    any_ = pl.BlockSpec(memory_space=pltpu.HBM)
    vmem = pl.BlockSpec(memory_space=pltpu.VMEM)
    dma = pltpu.SemaphoreType.DMA
    abuf, bbuf, c1 = pl.pallas_call(
        _kernel1,
        out_shape=(
            pltpu.VMEM((10, ROWS, KT), BF16),
            pltpu.VMEM((PANELS, DEPTH, PW), BF16),
            pltpu.HBM((FIRST, ROWS, PW), BF16),
        ),
        in_specs=[any_, any_],
        out_specs=(vmem, vmem, any_),
        scratch_shapes=[
            pltpu.VMEM((5, TRIP, PW), F32),
            pltpu.VMEM((2, TRIP, PW), BF16),
            dma((10,)),
            dma((PANELS,)),
            dma((2,)),
            dma((7, PANELS)),
            dma((7, PANELS)),
            dma((2, 2)),
        ],
        compiler_params=pltpu.CompilerParams(
            collective_id=0, has_side_effects=True, vmem_limit_bytes=GRANT
        ),
    )(a, b)
    abuf = pltpu.with_memory_space_constraint(abuf, pltpu.VMEM)
    bbuf = pltpu.with_memory_space_constraint(bbuf, pltpu.VMEM)
    c1 = pltpu.with_memory_space_constraint(c1, pltpu.HBM)
    return pl.pallas_call(
        _with_accs(_kernel2),
        out_shape=jax.ShapeDtypeStruct((ROWS, DEPTH), BF16),
        in_specs=[vmem, vmem, any_],
        out_specs=any_,
        scratch_shapes=[
            pltpu.VMEM((4, SLAB, PW), BF16),
            pltpu.VMEM((3, ROWS, PW), BF16),
            dma((4,)),
            dma((3,)),
            dma((3,)),
        ],
        compiler_params=pltpu.CompilerParams(vmem_limit_bytes=GRANT),
    )(abuf, bbuf, c1)


def solution(mesh):
    spec = P("fsdp", None)
    return jax.shard_map(_local, mesh=mesh, in_specs=(spec, spec), out_specs=spec, check_vma=False)
```

time: 178 us -> 103 us (0.58)
  Pallas kernels: 0 us -> 103 us
  matrix products: 90.2 us -> 0 us
  waiting for transfers between devices: 74 us -> 0 us
  between operations: 13.4 us -> 0.17 us
    pallas_call x0 -> x2, Pallas kernels: none -> 103 us  [the longest x1 75.2 us: _local(): pl.pallas_call(_kernel1, out_shape=(pltpu.VMEM((10, ROWS, KT), BF16), plt...]
    dot_general x1 -> x0, matrix products: 90.2 us -> none  [local_fn(): jnp.dot(left_blk, full_right, preferred_element_type=jnp.float32)]
    all_gather x1 -> x0, waiting for transfers between devices: 73.3 us -> none  [local_fn(): full_right = lax.all_gather(right_blk, 'fsdp', axis=0, tiled=True)]
  transfers between devices with their start and end apart: 1 -> 0, of which waited for: 1 -> 0; matrix products, arithmetic and copies ran while one was open for 0% -> 0% of each run, Pallas kernels for 0% -> 0%
where the time goes in v1:
time: 103 us
  Pallas kernels  103 us (100%)
    pallas_call x1, Pallas kernels, _local(): pl.pallas_call(_kernel1, out_shape=(pltpu.VMEM((10, ROWS, KT), BF16), plt...  75.2 us
    pallas_call x1, Pallas kernels, _local(): pl.pallas_call(_with_accs(_kernel2), out_shape=jax.ShapeDtypeStruct((ROWS...  27.7 us

profile of v1, /device:TPU:0, one launch (start us, length us, event | category | flops | bytes accessed | tf_op | source)
XLA Modules:
  0.0 103.1 jit_solution(6371503003032613206)
XLA Ops:
  0.0 75.2 %shard_map.28 = (bf16[10,6144,256]{2,1,0:T(8,128)(2,1)S(1)}, bf16[10,2560,256]{2,1,0:T(8,128)(2,1)S(1)}, bf16[7,6144,256]{2,1,0:T(8,128)(2,1)}) custom-call(bf16[6144,2560]{1,0:T(8,128)(2,1)} %a_ref.1, bf16[320,2560]{1,0:T(8,128)(2,1)} %b_ref.1), custom_call_target="tpu_custom_call" | custom-call | tf_op jit(solution)/shard_map/pallas_call | solution.py:423
  75.2 27.7 %shard_map.29 = bf16[6144,2560]{1,0:T(8,128)(2,1)} custom-call(bf16[10,6144,256]{2,1,0:T(8,128)(2,1)S(1)} %get-tuple-element.8.refs_0_, bf16[10,2560,256]{2,1,0:T(8,128)(2,1)S(1)} %get-tuple-element.9.refs_1_, bf16[7,6144,256]{2,1,0:T(8,128)(2,1)} %get-tuple-element.10.refs_2_), custom_call_target="tpu_custom_call" | custom-call | tf_op jit(solution)/shard_map/pallas_call | solution.py:449

commit v2 on v1

--- a/solution.py
+++ b/solution.py
@@ -20,7 +20,6 @@
 HALF = BLK // 2
 PART = 128
 FIRST = 7
-ACCP = 3
 GRANT = int(21.4 * 2**20)
 
 
@@ -135,7 +134,7 @@
     }
 
     def pair(part, dev):
-        lo, size = ((0, ACCP), (ACCP, PANELS - ACCP))[part]
+        lo, size = ((0, 1), (1, 2), (3, PANELS - 3))[part]
         piece = bbuf.at[pl.ds(lo, size), rows(dev)]
         return pltpu.make_async_remote_copy(
             src_ref=piece, dst_ref=piece, send_sem=psem.at[0, part], recv_sem=psem.at[1, part],
@@ -144,7 +143,12 @@
 
     def aload(i):
         cols = pl.ds(pl.multiple_of(kt[i] * KT, KT), KT)
-        return pltpu.make_async_copy(a_ref.at[:, cols], abuf.at[i], asem.at[i])
+        return pltpu.make_async_copy(a_ref.at[:, cols], abuf.at[i], asem.at[i - 2])
+
+    def aload_half(i, t):
+        cols = pl.ds(pl.multiple_of(kt[i] * KT, KT), KT)
+        part = pl.ds(t * TRIP, TRIP)
+        return pltpu.make_async_copy(a_ref.at[part, cols], abuf.at[i, part], asem.at[8 + 2 * t + i])
 
     def bload(n):
         return pltpu.make_async_copy(b_ref.at[:, pl.ds(n * PW, PW)], bbuf.at[n, rows(me)], bsem.at[n])
@@ -164,9 +168,9 @@
         recv[3](n).wait_recv()
         send[6](n).start()
 
-    def service1(n):
+    def service1(n, depth=2):
         arrived(n)
-        ahead(n + 2)
+        ahead(n + depth)
 
     def xy_ready(n):
         recv[4](n).wait_recv()
@@ -186,35 +190,34 @@
 
     def out_copy(g, panel, t):
         return pltpu.make_async_copy(
-            stage.at[g % 2], c1_ref.at[panel, pl.ds(pl.multiple_of(t * TRIP, TRIP), TRIP)], osem.at[g % 2]
+            stage.at[g % 4], c1_ref.at[panel, pl.ds(pl.multiple_of(t * TRIP, TRIP), TRIP)], osem.at[g % 4]
         )
 
-    def keep(n, poss, slot, t, add=False):
-        for s in range(3):
-            row = t * TRIP + s * SLAB
-            at = slice(s * SLAB, (s + 1) * SLAB)
-            value = product(n, row, poss)
-            psum[slot, at, :] = psum[slot, at, :] + value if add else value
-
-    def final(n, poss, slot, t):
-        g = 2 * n + t
-
-        @pl.when(g >= 2)
-        def _():
-            out_copy(g, 0, 0).wait()
-
-        for s in range(3):
-            row = t * TRIP + s * SLAB
-            value = product(n, row, poss)
-            if slot is not None:
-                value = psum[slot, s * SLAB : (s + 1) * SLAB, :] + value
-            stage[g % 2, s * SLAB : (s + 1) * SLAB, :] = value.astype(BF16)
-        out_copy(g, n, t).start()
-
-    def halves(body, between=None):
+    def keep(n, poss, slot, halves, add=False):
+        for t in halves:
+            for s in range(3):
+                row = t * TRIP + s * SLAB
+                at = pl.ds(pl.multiple_of(row, SLAB), SLAB)
+                value = product(n, row, poss)
+                psum[slot, at, :] = psum[slot, at, :] + value if add else value
+
+    def final(n, poss, slot, halves, wait):
+        if wait:
+            for t in halves:
+                out_copy(2 * n + t, 0, 0).wait()
+        for t in halves:
+            for s in range(3):
+                row = t * TRIP + s * SLAB
+                value = product(n, row, poss)
+                if slot is not None:
+                    value = psum[slot, pl.ds(pl.multiple_of(row, SLAB), SLAB), :] + value
+                stage[(2 * n + t) % 4, s * SLAB : (s + 1) * SLAB, :] = value.astype(BF16)
+        for t in halves:
+            out_copy(2 * n + t, n, t).start()
+
+    def split(body, between):
         def trip(t, _):
-            if between is not None:
-                pl.when(t == 1)(between)
+            pl.when(t == 1)(between)
             body(t)
             return 0
 
@@ -222,108 +225,102 @@
 
     for n in range(PANELS):
         bload(n).start()
-    for i in range(2):
-        aload(i).start()
+    for t in range(2):
+        for i in range(2):
+            aload_half(i, t).start()
     barrier = pltpu.get_barrier_semaphore()
     for dev in (other, xn, yn):
         pl.semaphore_signal(barrier, inc=1, device_id=(dev,), device_id_type=MESH)
     pl.semaphore_wait(barrier, 3)
     bload(0).wait()
+    pair(0, me).start()
     ahead(0)
     bload(1).wait()
     bload(2).wait()
-    pair(0, me).start()
     ahead(1)
+    pair(1, me).start()
     for n in range(3, PANELS):
         bload(n).wait()
-    pair(1, me).start()
+    pair(2, me).start()
 
     own, mid, far = [0, 1], [2, 3, 4, 5, 6], [7, 8, 9]
-    aload(0).wait()
-    aload(1).wait()
-    for i in range(2, 10):
-        aload(i).start()
+    both = (0, 1)
     pair(0, other).wait_recv()
-
-    def own_half(v, _):
-        @pl.when(v == 4)
-        def _():
-            service1(0)
-
-        keep(v // 2, own, v, v % 2)
-        return 0
-
-    lax.fori_loop(0, 5, own_half, 0)
+    for t in range(2):
+        for i in range(2):
+            aload_half(i, t).wait()
+        if t == 1:
+            for i in range(2, 10):
+                aload(i).start()
+        keep(0, own, 0, (t,))
+    pair(1, other).wait_recv()
+    keep(1, own, 1, both)
+    service1(0)
     for i in range(2, 7):
         aload(i).wait()
     xy_ready(0)
-    halves(lambda t: keep(0, mid, t, t, True))
-    service1(1)
+    split(lambda t: keep(0, mid, 0, (t,), True), lambda: service1(1))
     diagonal(0)
     xy_ready(1)
-    halves(lambda t: keep(1, mid, 2 + t, t, True))
+    keep(1, mid, 1, both, True)
     service1(2)
     for i in range(7, 10):
         aload(i).wait()
     d_ready(0)
-    halves(lambda t: final(0, far, t, t))
+    final(0, far, 0, both, False)
     diagonal(1)
     xy_ready(2)
-    keep(2, mid, 4, 0, True)
-    service1(3)
+    split(lambda t: keep(2, own + mid, 0, (t,)), lambda: service1(3))
+    diagonal(2)
     d_ready(1)
-    halves(lambda t: final(1, far, 2 + t, t), lambda: diagonal(2))
+    final(1, far, 1, both, False)
+    service1(4)
     d_ready(2)
-    final(2, far, 4, 0)
-    final(2, own + mid + far, None, 1)
-    service1(4)
-    xy_ready(3)
-    pair(1, other).wait_recv()
-    halves(lambda t: keep(3, own + mid, t, t), lambda: diagonal(3))
-    service1(5)
-    d_ready(3)
-    halves(lambda t: final(3, far, t, t), lambda: diagonal(4))
+    split(lambda t: final(2, far, 0, (t,), True), lambda: diagonal(3))
+    pair(2, other).wait_recv()
 
     def full_half(u, _):
-        n, t = 4 + u // 2, u % 2
+        n, t = 3 + u // 2, u % 2
 
         @pl.when(t == 0)
         def _():
             xy_ready(n)
             d_ready(n)
 
-        @pl.when((u >= 1) & (u <= 2))
-        def _():
-            service1(5 + u)
-            diagonal(4 + u)
-
-        @pl.when(u == 3)
-        def _():
-            arrived(8)
-
-        @pl.when(u == 4)
-        def _():
-            diagonal(7)
-
-        @pl.when(u == 5)
-        def _():
-            arrived(9)
+        @pl.when((u >= 1) & (u <= 3))
+        def _():
+            service1(4 + u)
+
+        @pl.when((u == 5) | (u == 6))
+        def _():
+            arrived(3 + u)
+
+        @pl.when(u == 1)
+        def _():
+            diagonal(4)
+
+        @pl.when((u >= 3) & (u <= 5))
+        def _():
+            diagonal(2 + u)
+
+        @pl.when(u == 7)
+        def _():
             diagonal(8)
-
-        final(n, own + mid + far, None, t)
+            diagonal(9)
+
+        final(n, own + mid + far, None, (t,), True)
         return 0
 
-    lax.fori_loop(0, 2 * (FIRST - 4), full_half, 0)
-    diagonal(9)
+    lax.fori_loop(0, 2 * (FIRST - 3), full_half, 0)
     for n in range(FIRST, PANELS):
         xy_ready(n)
         d_ready(n)
     for kind in range(7):
         for n in range(PANELS):
             send[kind](n).wait_send()
-    for part in range(2):
+    for part in range(3):
         pair(part, me).wait_send()
-    for g in range(2):
+    for g in range(4):
         out_copy(g, 0, 0).wait()
 
 
@@ -333,20 +330,20 @@
     poss = list(range(10))
 
     def load(u):
-        return pltpu.make_async_copy(c1_ref.at[u], move.at[u % 3], lsem.at[u % 3])
+        return pltpu.make_async_copy(c1_ref.at[u], move.at[u % 4], lsem.at[u % 4])
 
     def store(u):
         cols = pl.ds(pl.multiple_of(u * PW, PW), PW)
-        return pltpu.make_async_copy(move.at[u % 3], c_ref.at[:, cols], wsem.at[u % 3])
+        return pltpu.make_async_copy(move.at[u % 4], c_ref.at[:, cols], wsem.at[u % 4])
 
     def out_copy(tau):
         panel = FIRST + tau // SLABS
         return pltpu.make_async_copy(
-            stage.at[tau % 4],
+            stage.at[tau % 8],
             c_ref.at[
                 pl.ds(pl.multiple_of((tau % SLABS) * SLAB, SLAB), SLAB), pl.ds(pl.multiple_of(panel * PW, PW), PW)
             ],
-            osem.at[tau % 4],
+            osem.at[tau % 8],
         )
 
     load(0).start()
@@ -359,20 +356,18 @@
             load(u - 1).wait()
             store(u - 1).start()
 
-        @pl.when((u >= 3) & (u <= FIRST + 2))
-        def _():
-            store(u - 3).wait()
-
-        @pl.when((u >= 1) & (u < FIRST))
-        def _():
-            load(u).start()
-
-        for j in range(2):
-            tau = 2 * u + j - 1
-
-            @pl.when(tau >= 4)
+            @pl.when(u < FIRST)
             def _():
-                out_copy(tau - 4).wait()
+                @pl.when(u >= 4)
+                def _():
+                    store(u - 4).wait()
+
+                load(u).start()
+
+        @pl.when(u >= 4)
+        def _():
+            out_copy(2 * u - 8).wait()
+            out_copy(2 * u - 7).wait()
 
         reg = 0
         for j in range(2):
@@ -380,7 +375,7 @@
             panel = FIRST + tau // SLABS
             nextpanel = FIRST + ((tau + 1) // SLABS) % (PANELS - FIRST)
 
-            def emit(row, value, slot=(tau + 3) % 4):
+            def emit(row, value, slot=(tau + 7) % 8):
                 stage[slot, pl.ds(row, PART), :] = value.astype(BF16)
 
             reg = mxu.tile(j, tau % SLABS, panel, nextpanel, poss, reg, emit)
@@ -394,17 +389,16 @@
 
     lax.fori_loop(0, trips, trip, 0)
     last = 2 * trips - 1
-    out_copy(last - 4).wait()
 
     def emit(row, value):
-        stage[last % 4, pl.ds(row, PART), :] = value.astype(BF16)
+        stage[last % 8, pl.ds(row, PART), :] = value.astype(BF16)
 
     mxu.drain(1, emit)
     out_copy(last).start()
     mxu.drop(0)
-    for u in range(trips - 3, FIRST):
+    for u in range(FIRST - 4, FIRST):
         store(u).wait()
-    for tau in range(last - 3, last + 1):
+    for tau in range(2 * trips - 8, last + 1):
         out_copy(tau).wait()
 
 
@@ -430,14 +424,14 @@
         in_specs=[any_, any_],
         out_specs=(vmem, vmem, any_),
         scratch_shapes=[
-            pltpu.VMEM((5, TRIP, PW), F32),
-            pltpu.VMEM((2, TRIP, PW), BF16),
-            dma((10,)),
+            pltpu.VMEM((2, ROWS, PW), F32),
+            pltpu.VMEM((4, TRIP, PW), BF16),
+            dma((12,)),
             dma((PANELS,)),
-            dma((2,)),
+            dma((4,)),
             dma((7, PANELS)),
             dma((7, PANELS)),
-            dma((2, 2)),
+            dma((2, 3)),
         ],
         compiler_params=pltpu.CompilerParams(
             collective_id=0, has_side_effects=True, vmem_limit_bytes=GRANT
@@ -452,11 +446,11 @@
         in_specs=[vmem, vmem, any_],
         out_specs=any_,
         scratch_shapes=[
-            pltpu.VMEM((4, SLAB, PW), BF16),
-            pltpu.VMEM((3, ROWS, PW), BF16),
+            pltpu.VMEM((8, SLAB, PW), BF16),
+            pltpu.VMEM((4, ROWS, PW), BF16),
+            dma((8,)),
             dma((4,)),
-            dma((3,)),
-            dma((3,)),
+            dma((4,)),
         ],
         compiler_params=pltpu.CompilerParams(vmem_limit_bytes=GRANT),
     )(abuf, bbuf, c1)

time: 103 us -> 100 us (0.971)
  Pallas kernels: 103 us -> 99.7 us
    pallas_call x1, Pallas kernels: 75.2 us -> 72 us  [_local(): pl.pallas_call(_kernel1, out_shape=(pltpu.VMEM((10, ROWS, KT), BF16), plt...]
where the time goes in v2:
time: 100 us; the launch traced here: 99.9 us
  Pallas kernels  99.7 us (100%)
    pallas_call x1, Pallas kernels, _local(): pl.pallas_call(_kernel1, out_shape=(pltpu.VMEM((10, ROWS, KT), BF16), plt...  72 us
    pallas_call x1, Pallas kernels, _local(): pl.pallas_call(_with_accs(_kernel2), out_shape=jax.ShapeDtypeStruct((ROWS...  27.7 us

profile of v2, /device:TPU:0, one launch (start us, length us, event | category | flops | bytes accessed | tf_op | source)
XLA Modules:
  0.0 99.9 jit_solution(4734553921007478056)
XLA Ops:
  0.0 72.0 %shard_map.28 = (bf16[10,6144,256]{2,1,0:T(8,128)(2,1)S(1)}, bf16[10,2560,256]{2,1,0:T(8,128)(2,1)S(1)}, bf16[7,6144,256]{2,1,0:T(8,128)(2,1)}) custom-call(bf16[6144,2560]{1,0:T(8,128)(2,1)} %a_ref.1, bf16[320,2560]{1,0:T(8,128)(2,1)} %b_ref.1), custom_call_target="tpu_custom_call" | custom-call | tf_op jit(solution)/shard_map/pallas_call | solution.py:417
  72.0 27.7 %shard_map.29 = bf16[6144,2560]{1,0:T(8,128)(2,1)} custom-call(bf16[10,6144,256]{2,1,0:T(8,128)(2,1)S(1)} %get-tuple-element.8.refs_0_, bf16[10,2560,256]{2,1,0:T(8,128)(2,1)S(1)} %get-tuple-element.9.refs_1_, bf16[7,6144,256]{2,1,0:T(8,128)(2,1)} %get-tuple-element.10.refs_2_), custom_call_target="tpu_custom_call" | custom-call | tf_op jit(solution)/shard_map/pallas_call | solution.py:443

commit v3 on v2

--- a/solution.py
+++ b/solution.py
@@ -75,7 +75,7 @@
                 for p in range(4):
                     rows = pl.ds(pl.multiple_of(slab * SLAB + q * 512 + p * PART, PART), PART)
                     pltpu.matmul_acc_lhs(
-                        self.acc(rng, q, p), self.abuf[i, rows, :], load_staged_rhs=reg if p == 0 else None
+                        self.acc(rng, q, p), self.abuf[rows, i * KT : (i + 1) * KT], load_staged_rhs=reg if p == 0 else None
                     )
             reg = 1 - reg
             if k < n - 1:
@@ -141,14 +141,15 @@
             device_id=(other,), device_id_type=MESH,
         )
 
-    def aload(i):
-        cols = pl.ds(pl.multiple_of(kt[i] * KT, KT), KT)
-        return pltpu.make_async_copy(a_ref.at[:, cols], abuf.at[i], asem.at[i - 2])
-
-    def aload_half(i, t):
-        cols = pl.ds(pl.multiple_of(kt[i] * KT, KT), KT)
-        part = pl.ds(t * TRIP, TRIP)
-        return pltpu.make_async_copy(a_ref.at[part, cols], abuf.at[i, part], asem.at[8 + 2 * t + i])
+    groups = ((0, 2), (2, 3), (5, 2), (7, 3))
+
+    def aload(i, t):
+        first, count = groups[i]
+        cols = pl.ds(pl.multiple_of(kt[first] * KT, KT), count * KT)
+        part = pl.ds(pl.multiple_of(t * TRIP, TRIP), TRIP)
+        return pltpu.make_async_copy(
+            a_ref.at[part, cols], abuf.at[part, pl.ds(first * KT, count * KT)], asem.at[i, t]
+        )
 
     def bload(n):
         return pltpu.make_async_copy(b_ref.at[:, pl.ds(n * PW, PW)], bbuf.at[n, rows(me)], bsem.at[n])
@@ -182,7 +183,7 @@
     def product(n, row, poss):
         total = None
         for i in poss:
-            left = abuf[i, pl.ds(pl.multiple_of(row, SLAB), SLAB), :]
+            left = abuf[pl.ds(pl.multiple_of(row, SLAB), SLAB), i * KT : (i + 1) * KT]
             right = bbuf[n, pl.ds(pl.multiple_of(kt[i] * KT, KT), KT), :]
             part = jnp.dot(left, right, preferred_element_type=F32)
             total = part if total is None else total + part
@@ -190,16 +191,22 @@
 
     def out_copy(g, panel, t):
         return pltpu.make_async_copy(
-            stage.at[g % 4], c1_ref.at[panel, pl.ds(pl.multiple_of(t * TRIP, TRIP), TRIP)], osem.at[g % 4]
+            stage.at[g % 2], c1_ref.at[panel, pl.ds(pl.multiple_of(t * TRIP, TRIP), TRIP)], osem.at[g % 2]
         )
+
+    def held(slot, row):
+        return pl.ds(pl.multiple_of(slot * ROWS + row, SLAB), SLAB)
+
+    def scoped(fn):
+        pl.when(me >= 0)(fn)
 
     def keep(n, poss, slot, halves, add=False):
         for t in halves:
             for s in range(3):
                 row = t * TRIP + s * SLAB
-                at = pl.ds(pl.multiple_of(row, SLAB), SLAB)
+                at = held(slot, row)
                 value = product(n, row, poss)
-                psum[slot, at, :] = psum[slot, at, :] + value if add else value
+                psum[at, :] = psum[at, :] + value if add else value
 
     def final(n, poss, slot, halves, wait):
         if wait:
@@ -210,8 +217,8 @@
                 row = t * TRIP + s * SLAB
                 value = product(n, row, poss)
                 if slot is not None:
-                    value = psum[slot, pl.ds(pl.multiple_of(row, SLAB), SLAB), :] + value
-                stage[(2 * n + t) % 4, s * SLAB : (s + 1) * SLAB, :] = value.astype(BF16)
+                    value = psum[held(slot, row), :] + value
+                stage[(2 * n + t) % 2, s * SLAB : (s + 1) * SLAB, :] = value.astype(BF16)
         for t in halves:
             out_copy(2 * n + t, n, t).start()
 
@@ -226,8 +233,7 @@
     for n in range(PANELS):
         bload(n).start()
     for t in range(2):
-        for i in range(2):
-            aload_half(i, t).start()
+        aload(0, t).start()
     barrier = pltpu.get_barrier_semaphore()
     for dev in (other, xn, yn):
         pl.semaphore_signal(barrier, inc=1, device_id=(dev,), device_id_type=MESH)
@@ -247,36 +253,44 @@
     both = (0, 1)
     pair(0, other).wait_recv()
     for t in range(2):
-        for i in range(2):
-            aload_half(i, t).wait()
-        if t == 1:
-            for i in range(2, 10):
-                aload(i).start()
+        aload(0, t).wait()
+        for h in both:
+            for i in (1, 2) if t == 0 else (3,):
+                aload(i, h).start()
         keep(0, own, 0, (t,))
     pair(1, other).wait_recv()
     keep(1, own, 1, both)
     service1(0)
-    for i in range(2, 7):
-        aload(i).wait()
+    scoped(lambda: keep(2, own, 2, (0,)))
     xy_ready(0)
-    split(lambda t: keep(0, mid, 0, (t,), True), lambda: service1(1))
+
+    def first_mid(t):
+        aload(1, t).wait()
+        aload(2, t).wait()
+        keep(0, mid, 0, (t,), True)
+
+    split(first_mid, lambda: service1(1))
     diagonal(0)
     xy_ready(1)
     keep(1, mid, 1, both, True)
     service1(2)
-    for i in range(7, 10):
-        aload(i).wait()
+    for h in both:
+        aload(3, h).wait()
     d_ready(0)
     final(0, far, 0, both, False)
     diagonal(1)
     xy_ready(2)
-    split(lambda t: keep(2, own + mid, 0, (t,)), lambda: service1(3))
+    scoped(lambda: keep(2, mid, 2, (0,), True))
+    service1(3)
+    d_ready(1)
+    final(1, far, 1, both, True)
     diagonal(2)
-    d_ready(1)
-    final(1, far, 1, both, False)
     service1(4)
+    scoped(lambda: keep(2, own + mid, 0, (1,)))
     d_ready(2)
-    split(lambda t: final(2, far, 0, (t,), True), lambda: diagonal(3))
+    scoped(lambda: final(2, far, 2, (0,), True))
+    diagonal(3)
+    scoped(lambda: final(2, far, 0, (1,), True))
     pair(2, other).wait_recv()
 
     def full_half(u, _):
@@ -320,7 +334,7 @@
             send[kind](n).wait_send()
     for part in range(3):
         pair(part, me).wait_send()
-    for g in range(4):
+    for g in range(2):
         out_copy(g, 0, 0).wait()
 
 
@@ -417,18 +431,18 @@
     abuf, bbuf, c1 = pl.pallas_call(
         _kernel1,
         out_shape=(
-            pltpu.VMEM((10, ROWS, KT), BF16),
+            pltpu.VMEM((ROWS, DEPTH), BF16),
             pltpu.VMEM((PANELS, DEPTH, PW), BF16),
             pltpu.HBM((FIRST, ROWS, PW), BF16),
         ),
         in_specs=[any_, any_],
         out_specs=(vmem, vmem, any_),
         scratch_shapes=[
-            pltpu.VMEM((2, ROWS, PW), F32),
-            pltpu.VMEM((4, TRIP, PW), BF16),
-            dma((12,)),
+            pltpu.VMEM((2 * ROWS + TRIP, PW), F32),
+            pltpu.VMEM((2, TRIP, PW), BF16),
+            dma((4, 2)),
             dma((PANELS,)),
-            dma((4,)),
+            dma((2,)),
             dma((7, PANELS)),
             dma((7, PANELS)),
             dma((2, 3)),

time: 100 us -> 99.7 us (level)
  no operation moved by 1% of the time
where the time goes in v3:
time: 99.7 us; the launch traced here: 99.3 us
  Pallas kernels  99.2 us (99%)
    pallas_call x1, Pallas kernels, _local(): pl.pallas_call(_kernel1, out_shape=(pltpu.VMEM((ROWS, DEPTH), BF16), pltp...  71.4 us
    pallas_call x1, Pallas kernels, _local(): pl.pallas_call(_with_accs(_kernel2), out_shape=jax.ShapeDtypeStruct((ROWS...  27.7 us

profile of v3, /device:TPU:0, one launch (start us, length us, event | category | flops | bytes accessed | tf_op | source)
XLA Modules:
  0.0 99.3 jit_solution(8294012849749651679)
XLA Ops:
  0.0 71.4 %shard_map.28 = (bf16[6144,2560]{1,0:T(8,128)(2,1)S(1)}, bf16[10,2560,256]{2,1,0:T(8,128)(2,1)S(1)}, bf16[7,6144,256]{2,1,0:T(8,128)(2,1)}) custom-call(bf16[6144,2560]{1,0:T(8,128)(2,1)} %a_ref.1, bf16[320,2560]{1,0:T(8,128)(2,1)} %b_ref.1), custom_call_target="tpu_custom_call" | custom-call | tf_op jit(solution)/shard_map/pallas_call | solution.py:431
  71.4 27.7 %shard_map.29 = bf16[6144,2560]{1,0:T(8,128)(2,1)} custom-call(bf16[6144,2560]{1,0:T(8,128)(2,1)S(1)} %get-tuple-element.8.refs_0_, bf16[10,2560,256]{2,1,0:T(8,128)(2,1)S(1)} %get-tuple-element.9.refs_1_, bf16[7,6144,256]{2,1,0:T(8,128)(2,1)} %get-tuple-element.10.refs_2_), custom_call_target="tpu_custom_call" | custom-call | tf_op jit(solution)/shard_map/pallas_call | solution.py:457

commit v4 on v3

--- a/solution.py
+++ b/solution.py
@@ -286,6 +286,7 @@
     final(1, far, 1, both, True)
     diagonal(2)
     service1(4)
+    ahead(7)
     scoped(lambda: keep(2, own + mid, 0, (1,)))
     d_ready(2)
     scoped(lambda: final(2, far, 2, (0,), True))
@@ -301,9 +302,13 @@
             xy_ready(n)
             d_ready(n)
 
-        @pl.when((u >= 1) & (u <= 3))
-        def _():
-            service1(4 + u)
+        @pl.when((u == 1) | (u == 2))
+        def _():
+            service1(4 + u, 3)
+
+        @pl.when(u == 3)
+        def _():
+            arrived(7)
 
         @pl.when((u == 5) | (u == 6))
         def _():

time: 99.7 us -> 99.8 us (level)
  no operation moved by 1% of the time
where the time goes in v4:
time: 99.8 us; the launch traced here: 99.5 us
  Pallas kernels  99.3 us (99%)
    pallas_call x1, Pallas kernels, _local(): pl.pallas_call(_kernel1, out_shape=(pltpu.VMEM((ROWS, DEPTH), BF16), pltp...  71.6 us
    pallas_call x1, Pallas kernels, _local(): pl.pallas_call(_with_accs(_kernel2), out_shape=jax.ShapeDtypeStruct((ROWS...  27.7 us

profile of v4, /device:TPU:0, one launch (start us, length us, event | category | flops | bytes accessed | tf_op | source)
XLA Modules:
  0.0 99.5 jit_solution(8548742424585265939)
XLA Ops:
  0.0 71.6 %shard_map.28 = (bf16[6144,2560]{1,0:T(8,128)(2,1)S(1)}, bf16[10,2560,256]{2,1,0:T(8,128)(2,1)S(1)}, bf16[7,6144,256]{2,1,0:T(8,128)(2,1)}) custom-call(bf16[6144,2560]{1,0:T(8,128)(2,1)} %a_ref.1, bf16[320,2560]{1,0:T(8,128)(2,1)} %b_ref.1), custom_call_target="tpu_custom_call" | custom-call | tf_op jit(solution)/shard_map/pallas_call | solution.py:436
  71.6 27.7 %shard_map.29 = bf16[6144,2560]{1,0:T(8,128)(2,1)} custom-call(bf16[6144,2560]{1,0:T(8,128)(2,1)S(1)} %get-tuple-element.8.refs_0_, bf16[10,2560,256]{2,1,0:T(8,128)(2,1)S(1)} %get-tuple-element.9.refs_1_, bf16[7,6144,256]{2,1,0:T(8,128)(2,1)} %get-tuple-element.10.refs_2_), custom_call_target="tpu_custom_call" | custom-call | tf_op jit(solution)/shard_map/pallas_call | solution.py:462
